TPU v7x, 32 devices: a whole 2x2x4 slice. The times are simulated.
32 devices in a mesh: groups: 2 (over x), exp: 16 (over z, y, core).
Axes of the slice: x: 2, y: 2, z: 4, core: 2. Of those that a mesh axis runs over, the one named last changes fastest.
Arguments:
- cutouts: float32 [64, 12, 20736], P(('groups', 'exp')), parts along dimension 0, may hold values from -6 to 6
- variance: bfloat16 [64, 12, 20736], P(('groups', 'exp')), parts along dimension 0, may hold values from 0.1 to 30
- offsets: int32 [64, 12, 2], P(('groups', 'exp')), parts along dimension 0, may hold values from 0 to 15
- correlation_tiles: int32 [64, 12], P(('groups', 'exp')), parts along dimension 0, may hold values from 0 to 63, as said below
- slot_valid: int32 [64, 12], P(('groups', 'exp')), parts along dimension 0, may hold values from 0 to 1, as said below
- tile_slot: int32 [128], P('groups'), parts along dimension 0, may hold values from 0 to 63, as said below
Outputs:
- coadd: float32 [128, 128, 128], P(('groups', 'exp')), parts along dimension 0
- depth: float32 [128, 128, 128], P(('groups', 'exp')), parts along dimension 0
There are 2 independent parts, one for each index of `groups`. A program takes and returns all parts, laid end to end along the dimension named above; each array names one. Nothing has to cross between parts.
Inputs may be any that keep to these rules, and one draw needn't show every extreme that they name: `correlation_tiles`: the tile with id t is owned by the device of index tile_slot[t] // 4 along exp. Among the valid slots of one device's 2 exposures at most 3 name tiles of one owner; in every draw one owner is named exactly 3 times by the valid slots of every device. `slot_valid`: each exposure's valid slots come first; at least 6 of its 12 slots are valid. A permutation: tile t is stored in row tile_slot[t] of the outputs.
All inputs are finite; a program needn't handle non-finite values.
Results may differ from a plain program's by a relative error of at most 0.0003.
Values sent between devices are 32-bit elements; how exact they have to be, the bound alone decides.
A program may use at most 128 MiB of HBM per device.

v0:
```python
import functools

import jax
import jax.numpy as jnp
import numpy as np
from jax import lax
from jax.experimental import pallas as pl
from jax.experimental.pallas import tpu as pltpu
from jax.sharding import PartitionSpec as P

P_SIZE = 128
CP = 144
NOFF = 16
TAPS = 6
FIRST = 6
LANES = 128
ROWS = 8
PAD = 16
PARTS = 2
LAGS = 3
SWAP_EVERY = 4
clip_ratio = 1.5
MESH = pl.DeviceIdType.MESH


def tap_table():
    spread = 8.0 + np.arange(NOFF)[:, None] / NOFF - (FIRST + np.arange(TAPS))[None, :]
    table = np.where(np.abs(spread) < 3.0, np.sinc(spread) * np.sinc(spread / 3.0), 0.0)
    return table.astype(np.float32)


TABLE = tap_table()


def pick_taps(offset):
    taps = []
    for t in range(TAPS):
        value = jnp.zeros(offset.shape, jnp.float32)
        for o in range(NOFF):
            value = jnp.where(offset == o, float(TABLE[o, t]), value)
        taps.append(value)
    return taps


def coadd_kernel(
    dev_count, bits, cut_hbm, var_hbm, off_ref, tile_ref, valid_ref, slot_ref,
    coadd_ref, depth_ref, cut_ref, var_ref, weight_src, weight_got, taps_ref,
    cut_mid, var_mid, pick_wide, pick_ref, parts_ref, partial_ref, *rest,
):
    got_refs = rest[:bits]
    load_sem, weight_send, weight_recv, send_sem, recv_sem = rest[bits:]
    slots, exps, _ = cut_hbm.shape
    rows = slots * exps
    slot_total = slot_ref.shape[1]
    tile_dev = slot_total // dev_count
    width = ROWS * P_SIZE
    chunks = P_SIZE // ROWS
    span = ROWS * CP
    ring = partial_ref.shape[0]
    pad = pick_wide.shape[0] // (2 * PARTS)
    me = lax.axis_index("exp")

    barrier = pltpu.get_barrier_semaphore()

    @pl.loop(1, dev_count)
    def _(i):
        pl.semaphore_signal(
            barrier, inc=1, device_id={"exp": lax.rem(me + i, dev_count)}, device_id_type=MESH
        )

    def load(kind, s):
        source, to = ((cut_hbm, cut_ref), (var_hbm, var_ref))[kind]
        return pltpu.make_async_copy(
            source.at[s], to.at[pl.ds(s * exps, exps)], load_sem.at[kind, s]
        )

    for kind in (1, 0):
        for s in range(slots):
            load(kind, s).start()

    of_row = lax.broadcasted_iota(jnp.int32, (rows, slots), 0)
    of_slot = lax.broadcasted_iota(jnp.int32, (rows, slots), 1) == of_row // exps

    def by_row(values):
        column = jnp.zeros((rows, slots), jnp.float32)
        for e in range(exps):
            here = of_slot & (of_row % exps == e)
            column = column + jnp.where(here, values[e].astype(jnp.float32), 0.0)
        return jnp.sum(column, axis=1, keepdims=True)

    valid = by_row([valid_ref[e : e + 1, :] for e in range(exps)])
    tile = by_row([tile_ref[e : e + 1, :] for e in range(exps)])
    offsets = [by_row([off_ref[e, axis : axis + 1, :] for e in range(exps)]) for axis in range(2)]

    for s in range(slots):
        load(1, s).wait()

    def add_up(g, total):
        var = var_ref[:, pl.ds(pl.multiple_of(g * span, LANES), span)].astype(jnp.float32)
        for k in range(span // LANES):
            total = total + var[:, k * LANES : (k + 1) * LANES]
        return total

    sums = lax.fori_loop(0, CP // ROWS, add_up, jnp.zeros((rows, LANES), jnp.float32))

    exposure = lax.broadcasted_iota(jnp.int32, (rows, 1), 0) % exps
    row_total = jnp.sum(sums, axis=1, keepdims=True) * valid
    own = []
    for e in range(exps):
        total = jnp.sum(jnp.where(exposure == e, row_total, 0.0), axis=0, keepdims=True)
        count = jnp.sum(jnp.where(exposure == e, valid, 0.0), axis=0, keepdims=True)
        own.append(1.0 / (total / (count * (CP * CP))))
    own_sum = functools.reduce(lambda a, b: a + b, own)
    weight_src[...] = jnp.broadcast_to(own_sum, weight_src.shape)
    pl.semaphore_wait(barrier, dev_count - 1)

    def weight_copy(i):
        return pltpu.make_async_remote_copy(
            src_ref=weight_src,
            dst_ref=weight_got.at[i],
            send_sem=weight_send.at[i],
            recv_sem=weight_recv.at[i],
            device_id={"exp": lax.rem(me + i, dev_count)},
            device_id_type=MESH,
        )

    @pl.loop(1, dev_count)
    def _(i):
        weight_copy(i).start()

    for axis in range(2):
        taps = pick_taps(jnp.broadcast_to(offsets[axis], (rows, LANES)))
        for t in range(TAPS):
            taps_ref[axis, 0, t] = taps[t]
            taps_ref[axis, 1, t] = taps[t] * taps[t]

    def columns(g):
        at = pl.ds(pl.multiple_of(g * span, LANES), span)
        for kind in range(2):
            data = (cut_ref, var_ref)[kind][:, at].astype(jnp.float32)
            mid = (cut_mid, var_mid)[kind]
            for r in range(ROWS):
                start = r * CP + FIRST
                got = taps_ref[1, kind, 0] * data[:, start : start + LANES]
                for t in range(1, TAPS):
                    got = got + taps_ref[1, kind, t] * data[:, start + t : start + t + LANES]
                mid[:, pl.ds(pl.multiple_of((g * ROWS + r) * LANES, LANES), LANES)] = got

    row = lax.broadcasted_iota(jnp.int32, (rows, 2 * slot_total), 1)
    place = row // (2 * tile_dev)
    kind_of = (row // tile_dev) % 2
    tile_ids = lax.broadcasted_iota(jnp.int32, (rows, slot_total), 1)
    storage = jnp.sum(
        jnp.where(tile == tile_ids.astype(jnp.float32), slot_ref[...].astype(jnp.float32), 0.0),
        axis=1,
        keepdims=True,
    )
    pick_wide[...] = jnp.zeros_like(pick_wide)
    parts_ref[...] = jnp.zeros_like(parts_ref)
    for variant in range(2):
        order = list(range(bits))
        if variant == 1 and bits >= 3:
            order[1], order[2] = 2, 1
        owner = jnp.zeros_like(place)
        for b in range(bits):
            owner = owner + ((place // (1 << (bits - 1 - b))) % 2) * (1 << order[b])
        wanted = (owner * tile_dev + row % tile_dev).astype(jnp.float32)
        for kind in range(2):
            hit = jnp.where((kind_of == kind) & (wanted == storage), valid, 0.0)
            for part in range(PARTS):
                base = (kind * PARTS + part) * pad
                pick_wide[base : base + rows, :] = hit
        pick_ref[variant] = pick_wide[...].T.astype(jnp.bfloat16)

    for s in range(slots):
        load(0, s).wait()

    columns(0)
    columns(1)

    @pl.loop(1, dev_count)
    def _(i):
        weight_copy(i).wait()

    weight_got[0] = weight_src[...]
    average = jnp.sum(weight_got[...], axis=0)[0:1, 0:1] / (exps * dev_count)
    factor = jnp.zeros((rows, 1), jnp.float32)
    for e in range(exps):
        factor = jnp.where(exposure == e, jnp.minimum(own[e], clip_ratio * average) / own[e], factor)

    def swapped(c):
        return lax.div(lax.rem(c + SWAP_EVERY - 2, SWAP_EVERY), SWAP_EVERY - 1)

    def stride_of(b, c):
        if bits >= 3 and b == 1:
            return 2 + 2 * swapped(c)
        if bits >= 3 and b == 2:
            return 4 - 2 * swapped(c)
        return 1 << b

    def bit_of(b, c):
        return lax.rem(lax.div(me, stride_of(b, c)), 2)

    def block_copy(b, c):
        n = dev_count >> (b + 1)
        bit = bit_of(b, c)
        if b == 0:
            source = partial_ref.at[lax.rem(c, ring), pl.ds((1 - bit) * n, n)]
        else:
            source = got_refs[b - 1].at[c, pl.ds((1 - bit) * n, n)]
        return pltpu.make_async_remote_copy(
            src_ref=source,
            dst_ref=got_refs[b].at[c],
            send_sem=send_sem.at[b, c],
            recv_sem=recv_sem.at[b, c],
            device_id={"exp": me + (1 - 2 * bit) * stride_of(b, c)},
            device_id_type=MESH,
        )

    def kept(b, c):
        n = dev_count >> (b + 1)
        if b == 0:
            return partial_ref[lax.rem(c, ring), pl.ds(bit_of(b, c) * n, n)]
        return got_refs[b - 1][c, pl.ds(bit_of(b, c) * n, n)]

    @pl.loop(0, chunks + LAGS * bits - LAGS + 1)
    def _(step):
        @pl.when(step < chunks)
        def _():
            c = step
            columns(c + 2)
            for r in range(ROWS):
                value = []
                for kind in range(2):
                    mid = (cut_mid, var_mid)[kind]
                    got = None
                    for t in range(TAPS):
                        from_row = c * ROWS + r + FIRST + t
                        at = pl.ds(pl.multiple_of(from_row * LANES, LANES), LANES)
                        term = taps_ref[0, kind, t] * mid[:, at]
                        got = term if t == 0 else got + term
                    value.append(got)
                inverse = 1.0 / value[1]
                scaled = value[0] * inverse
                for kind in range(2):
                    piece_of = (scaled, inverse)[kind] * factor
                    for part in range(PARTS):
                        base = (kind * PARTS + part) * pad
                        piece = piece_of.astype(jnp.bfloat16)
                        parts_ref[base : base + rows, r * LANES : (r + 1) * LANES] = piece
                        piece_of = piece_of - piece.astype(jnp.float32)

            @pl.when(c >= ring)
            def _():
                block_copy(0, c - ring).wait_send()

            added = jnp.dot(
                pick_ref[swapped(c)], parts_ref[...], preferred_element_type=jnp.float32
            )
            partial_ref[lax.rem(c, ring)] = added.reshape(dev_count, 2 * tile_dev, width)
            block_copy(0, c).start()

        for b in range(1, bits + 1):
            c = step - (LAGS * (b - 1) + 1)

            @pl.when((c >= 0) & (c < chunks))
            def _(b=b, c=c):
                block_copy(b - 1, c).wait_recv()
                total = got_refs[b - 1][c] + kept(b - 1, c)
                if b < bits:
                    got_refs[b - 1][c] = total
                    block_copy(b, c).start()
                else:
                    at = pl.ds(pl.multiple_of(c * width, LANES), width)
                    numerator = total[0, :tile_dev]
                    denominator = total[0, tile_dev:]
                    positive = denominator > 0
                    coadd_ref[:, at] = jnp.where(
                        positive, numerator / jnp.where(positive, denominator, 1.0), 0.0
                    )
                    depth_ref[:, at] = denominator

    @pl.loop(chunks - ring, chunks)
    def _(c):
        block_copy(0, c).wait_send()

    @pl.loop(0, chunks)
    def _(c):
        for b in range(1, bits):
            block_copy(b, c).wait_send()


def shards(cutouts, variance, offsets, correlation_tiles, slot_valid, tile_slot):
    dev_count = lax.axis_size("exp")
    exps, slots, pixels = cutouts.shape
    rows = exps * slots
    tile_total = tile_slot.shape[0]
    tile_dev = tile_total // dev_count
    bits = dev_count.bit_length() - 1
    chunks = P_SIZE // ROWS
    width = ROWS * P_SIZE
    ring = min(chunks, 4)
    depth = 2 * PARTS * (-(-rows // PAD) * PAD)
    area = P_SIZE * P_SIZE

    whole = pl.BlockSpec(memory_space=pltpu.VMEM)
    far = pl.BlockSpec(memory_space=pltpu.HBM)
    coadd, depth_sum = pl.pallas_call(
        functools.partial(coadd_kernel, dev_count, bits),
        out_shape=(jax.ShapeDtypeStruct((tile_dev, area), jnp.float32),) * 2,
        in_specs=[far] * 2 + [whole] * 4,
        out_specs=(whole,) * 2,
        scratch_shapes=[
            pltpu.VMEM((rows, pixels), cutouts.dtype),
            pltpu.VMEM((rows, pixels), variance.dtype),
            pltpu.VMEM((ROWS, LANES), jnp.float32),
            pltpu.VMEM((dev_count, ROWS, LANES), jnp.float32),
            pltpu.VMEM((2, 2, TAPS, rows, LANES), jnp.float32),
            pltpu.VMEM((rows, CP * P_SIZE), jnp.float32),
            pltpu.VMEM((rows, CP * P_SIZE), jnp.float32),
            pltpu.VMEM((depth, 2 * tile_total), jnp.float32),
            pltpu.VMEM((2, 2 * tile_total, depth), jnp.bfloat16),
            pltpu.VMEM((depth, width), jnp.bfloat16),
            pltpu.VMEM((ring, dev_count, 2 * tile_dev, width), jnp.float32),
        ]
        + [
            pltpu.VMEM((chunks, dev_count >> (b + 1), 2 * tile_dev, width), jnp.float32)
            for b in range(bits)
        ]
        + [
            pltpu.SemaphoreType.DMA((2, slots)),
            pltpu.SemaphoreType.DMA((dev_count,)),
            pltpu.SemaphoreType.DMA((dev_count,)),
            pltpu.SemaphoreType.DMA((bits, chunks)),
            pltpu.SemaphoreType.DMA((bits, chunks)),
        ],
        compiler_params=pltpu.CompilerParams(
            collective_id=0, has_side_effects=True, vmem_limit_bytes=60 * 1024 * 1024
        ),
        name="coadd",
    )(
        jnp.swapaxes(cutouts, 0, 1),
        jnp.swapaxes(variance, 0, 1),
        jnp.swapaxes(offsets, 1, 2),
        correlation_tiles,
        slot_valid,
        tile_slot.reshape(1, tile_total),
    )
    shape = (tile_dev, P_SIZE, P_SIZE)
    return (coadd.reshape(shape), depth_sum.reshape(shape))


def solution(mesh):
    in_specs = (
        P(("groups", "exp"), None, None),
        P(("groups", "exp"), None, None),
        P(("groups", "exp"), None, None),
        P(("groups", "exp"), None),
        P(("groups", "exp"), None),
        P("groups"),
    )
    out_specs = (P(("groups", "exp"), None, None), P(("groups", "exp"), None, None))
    return jax.shard_map(shards, mesh=mesh, in_specs=in_specs, out_specs=out_specs, check_vma=False)
```

profile of v0, /device:TPU:0, one launch (start us, length us, event | category | flops | bytes accessed | tf_op | source)
XLA Modules:
  0.0 66.5 jit_solution(6489068199745356650)
XLA Ops:
  0.6 64.0 %coadd.1 = (f32[4,16384]{1,0:T(4,128)}, f32[4,16384]{1,0:T(4,128)}) custom-call(f32[12,2,20736]{2,1,0:T(2,128)} %bitcast.10, bf16[12,2,20736]{2,1,0:T(2,128)(2,1)} %bitcast.11, s32[2,2,12]{2,1,0:T(2,128)} %bitcast.14, s32[2,12]{1,0:T(2,128)} %tile_ref.1, s32[2,12]{1,0:T(2,128)} %valid_ref.1, s32[1,64]{1,0:T(1,128)} %bitcast.15), custom_call_target="tpu_custom_call" | custom-call | tf_op jit(solution)/shard_map/coadd/pallas_call | solution.py:308
  64.6 1.9 %copy_bitcast_fusion = (f32[4,128,128]{2,1,0:T(8,128)}, f32[4,128,128]{2,1,0:T(8,128)}) fusion(f32[1,4,128,128]{3,1,2,0:T(4,128)} %bitcast.13, f32[1,4,128,128]{3,1,2,0:T(4,128)} %bitcast.12), kind=kLoop, calls=%fused_computation | loop fusion | bytes 1048576 | tf_op jit(solution)/shard_map/reshape | solution.py:350
where the time goes:
time: 66.7 us; the launch traced here: 66.5 us
  Pallas kernels  64 us (96%)
  local copies, waits for them, and re-layouts  1.85 us (3%)
    pallas_call x1, Pallas kernels, shards(): pl.pallas_call(functools.partial(coadd_kernel, dev_count, bits), out_shap...  64 us
    reshape x1, local copies, waits for them, and re-layouts, shards(): return (coadd.reshape(shape), depth_sum.reshape(shape))  1.85 us

commit v1 on v0

--- a/solution.py
+++ b/solution.py
@@ -19,6 +19,7 @@
 PARTS = 2
 LAGS = 3
 SWAP_EVERY = 4
+VMEM_LIMIT = 55_800_000
 clip_ratio = 1.5
 MESH = pl.DeviceIdType.MESH
 
@@ -43,7 +44,7 @@
 
 
 def coadd_kernel(
-    dev_count, bits, cut_hbm, var_hbm, off_ref, tile_ref, valid_ref, slot_ref,
+    dev_count, bits, slot_total, cut_hbm, var_hbm, small_ref,
     coadd_ref, depth_ref, cut_ref, var_ref, weight_src, weight_got, taps_ref,
     cut_mid, var_mid, pick_wide, pick_ref, parts_ref, partial_ref, *rest,
 ):
@@ -51,7 +52,6 @@
     load_sem, weight_send, weight_recv, send_sem, recv_sem = rest[bits:]
     slots, exps, _ = cut_hbm.shape
     rows = slots * exps
-    slot_total = slot_ref.shape[1]
     tile_dev = slot_total // dev_count
     width = ROWS * P_SIZE
     chunks = P_SIZE // ROWS
@@ -88,9 +88,12 @@
             column = column + jnp.where(here, values[e].astype(jnp.float32), 0.0)
         return jnp.sum(column, axis=1, keepdims=True)
 
-    valid = by_row([valid_ref[e : e + 1, :] for e in range(exps)])
-    tile = by_row([tile_ref[e : e + 1, :] for e in range(exps)])
-    offsets = [by_row([off_ref[e, axis : axis + 1, :] for e in range(exps)]) for axis in range(2)]
+    def small_row(i):
+        return small_ref[i : i + 1, :slots]
+
+    offsets = [by_row([small_row(2 * e + axis) for e in range(exps)]) for axis in range(2)]
+    tile = by_row([small_row(2 * exps + e) for e in range(exps)])
+    valid = by_row([small_row(3 * exps + e) for e in range(exps)])
 
     for s in range(slots):
         load(1, s).wait()
@@ -151,7 +154,7 @@
     kind_of = (row // tile_dev) % 2
     tile_ids = lax.broadcasted_iota(jnp.int32, (rows, slot_total), 1)
     storage = jnp.sum(
-        jnp.where(tile == tile_ids.astype(jnp.float32), slot_ref[...].astype(jnp.float32), 0.0),
+        jnp.where(tile == tile_ids.astype(jnp.float32), small_ref[4 * exps : 4 * exps + 1, :slot_total].astype(jnp.float32), 0.0),
         axis=1,
         keepdims=True,
     )
@@ -303,12 +306,25 @@
     depth = 2 * PARTS * (-(-rows // PAD) * PAD)
     area = P_SIZE * P_SIZE
 
+    lanes = max(LANES, tile_total)
+    small = jnp.concatenate(
+        [
+            jnp.pad(a, ((0, 0), (0, lanes - a.shape[1])))
+            for a in (
+                jnp.swapaxes(offsets, 1, 2).reshape(2 * exps, slots),
+                correlation_tiles,
+                slot_valid,
+                tile_slot.reshape(1, tile_total),
+            )
+        ],
+        axis=0,
+    )
     whole = pl.BlockSpec(memory_space=pltpu.VMEM)
     far = pl.BlockSpec(memory_space=pltpu.HBM)
     coadd, depth_sum = pl.pallas_call(
-        functools.partial(coadd_kernel, dev_count, bits),
+        functools.partial(coadd_kernel, dev_count, bits, tile_total),
         out_shape=(jax.ShapeDtypeStruct((tile_dev, area), jnp.float32),) * 2,
-        in_specs=[far] * 2 + [whole] * 4,
+        in_specs=[far] * 2 + [whole],
         out_specs=(whole,) * 2,
         scratch_shapes=[
             pltpu.VMEM((rows, pixels), cutouts.dtype),
@@ -335,16 +351,13 @@
             pltpu.SemaphoreType.DMA((bits, chunks)),
         ],
         compiler_params=pltpu.CompilerParams(
-            collective_id=0, has_side_effects=True, vmem_limit_bytes=60 * 1024 * 1024
+            collective_id=0, has_side_effects=True, vmem_limit_bytes=VMEM_LIMIT
         ),
         name="coadd",
     )(
         jnp.swapaxes(cutouts, 0, 1),
         jnp.swapaxes(variance, 0, 1),
-        jnp.swapaxes(offsets, 1, 2),
-        correlation_tiles,
-        slot_valid,
-        tile_slot.reshape(1, tile_total),
+        small,
     )
     shape = (tile_dev, P_SIZE, P_SIZE)
     return (coadd.reshape(shape), depth_sum.reshape(shape))

time: 66.7 us -> 64.9 us (0.973)
  Pallas kernels: 64 us -> 62.5 us
  local copies, waits for them, and re-layouts: 1.85 us -> 0.82 us
  other arithmetic: 0 us -> 0.74 us
    pallas_call x1, Pallas kernels: 64 us -> 62.5 us  [shards(): pl.pallas_call(functools.partial(coadd_kernel, dev_count, bits, tile_tota...]
    reshape x1, local copies, waits for them, and re-layouts: 1.85 us -> 0.82 us  [shards(): return (coadd.reshape(shape), depth_sum.reshape(shape))]
    concatenate x0 -> x1, other arithmetic: none -> 0.74 us  [shards(): jnp.concatenate([jnp.pad(a, ((0, 0), (0, lanes - a.shape[1]))) for a in (...]
where the time goes in v1:
time: 64.9 us; the launch traced here: 64.7 us
  Pallas kernels  62.5 us (96%)
  local copies, waits for them, and re-layouts  0.82 us (1%)
  other arithmetic  0.74 us (1%)
    pallas_call x1, Pallas kernels, shards(): pl.pallas_call(functools.partial(coadd_kernel, dev_count, bits, tile_tota...  62.5 us

profile of v1, /device:TPU:0, one launch (start us, length us, event | category | flops | bytes accessed | tf_op | source)
XLA Modules:
  0.0 64.7 jit_solution(9144206005488346586)
XLA Ops:
  0.6 0.7 %pad_add_fusion.small_ref = s32[9,128]{1,0:T(8,128)S(1)} fusion(s32[1,64]{1,0:T(1,128)} %bitcast.17, s32[2,12]{1,0:T(2,128)} %param.10, s32[2,12]{1,0:T(2,128)} %param.9, s32[4,12]{1,0:T(4,128)} %bitcast.16), kind=kLoop, calls=%fused_computation.2 | loop fusion | flops 3456 | bytes 5248 | tf_op jit(solution)/shard_map/concatenate | solution.py:310
  1.4 62.5 %coadd.1 = (f32[4,16384]{1,0:T(4,128)S(1)}, f32[4,16384]{1,0:T(4,128)S(1)}) custom-call(f32[12,2,20736]{2,1,0:T(2,128)} %bitcast.14, bf16[12,2,20736]{2,1,0:T(2,128)(2,1)} %bitcast.15, s32[9,128]{1,0:T(8,128)S(1)} %pad_add_fusion.small_ref), custom_call_target="tpu_custom_call" | custom-call | tf_op jit(solution)/shard_map/coadd/pallas_call | solution.py:324
  63.9 0.8 %copy_bitcast_fusion = (f32[4,128,128]{2,1,0:T(8,128)}, f32[4,128,128]{2,1,0:T(8,128)}) fusion(f32[1,4,128,128]{3,1,2,0:T(4,128)S(1)} %bitcast.13, f32[1,4,128,128]{3,1,2,0:T(4,128)S(1)} %bitcast.12), kind=kLoop, calls=%fused_computation | loop fusion | bytes 1048576 | tf_op jit(solution)/shard_map/reshape | solution.py:363

commit v2 on v1

--- a/solution.py
+++ b/solution.py
@@ -17,8 +17,12 @@
 ROWS = 8
 PAD = 16
 PARTS = 2
-LAGS = 3
-SWAP_EVERY = 4
+ALL_RING = 16
+AHEAD = 4
+LATE = (1,)
+LAGS = (1, 4, 8, 20)
+LATE_LAGS = (1, 3, 7, 16)
+LAST_PER_STEP = 3
 VMEM_LIMIT = 55_800_000
 clip_ratio = 1.5
 MESH = pl.DeviceIdType.MESH
@@ -43,13 +47,18 @@
     return taps
 
 
+def stage_lags(lags, bits):
+    middle = [lags[2] + 4 * i for i in range(bits - 3)]
+    return list(lags[:2]) + middle + [middle[-1] + lags[3] - lags[2]]
+
+
 def coadd_kernel(
     dev_count, bits, slot_total, cut_hbm, var_hbm, small_ref,
     coadd_ref, depth_ref, cut_ref, var_ref, weight_src, weight_got, taps_ref,
-    cut_mid, var_mid, pick_wide, pick_ref, parts_ref, partial_ref, *rest,
+    cut_mid, var_mid, value_ref, pick_wide, pick_ref, parts_ref, partial_ref, *rest,
 ):
     got_refs = rest[:bits]
-    load_sem, weight_send, weight_recv, send_sem, recv_sem = rest[bits:]
+    load_sem, weight_send, weight_recv, send_sem, recv_sem, last_send, last_recv = rest[bits:]
     slots, exps, _ = cut_hbm.shape
     rows = slots * exps
     tile_dev = slot_total // dev_count
@@ -59,6 +68,9 @@
     ring = partial_ref.shape[0]
     pad = pick_wide.shape[0] // (2 * PARTS)
     me = lax.axis_index("exp")
+
+    def bit_order(late):
+        return [0, *range(2, bits), 1] if late else list(range(bits))
 
     barrier = pltpu.get_barrier_semaphore()
 
@@ -160,26 +172,48 @@
     )
     pick_wide[...] = jnp.zeros_like(pick_wide)
     parts_ref[...] = jnp.zeros_like(parts_ref)
-    for variant in range(2):
-        order = list(range(bits))
-        if variant == 1 and bits >= 3:
-            order[1], order[2] = 2, 1
+    for late in range(2):
+        order = bit_order(late)
         owner = jnp.zeros_like(place)
         for b in range(bits):
-            owner = owner + ((place // (1 << (bits - 1 - b))) % 2) * (1 << order[b])
+            apart = (place // (1 << (bits - 1 - b))) % 2
+            mine = lax.rem(lax.div(me, 1 << order[b]), 2)
+            owner = owner + ((apart + mine) % 2) * (1 << order[b])
         wanted = (owner * tile_dev + row % tile_dev).astype(jnp.float32)
         for kind in range(2):
             hit = jnp.where((kind_of == kind) & (wanted == storage), valid, 0.0)
             for part in range(PARTS):
                 base = (kind * PARTS + part) * pad
                 pick_wide[base : base + rows, :] = hit
-        pick_ref[variant] = pick_wide[...].T.astype(jnp.bfloat16)
+        pick_ref[late] = pick_wide[...].T.astype(jnp.bfloat16)
 
     for s in range(slots):
         load(0, s).wait()
 
+    def resample(c):
+        for r in range(ROWS):
+            value = []
+            for kind in range(2):
+                mid = (cut_mid, var_mid)[kind]
+                got = None
+                for t in range(TAPS):
+                    from_row = c * ROWS + r + FIRST + t
+                    at = pl.ds(pl.multiple_of(from_row * LANES, LANES), LANES)
+                    term = taps_ref[0, kind, t] * mid[:, at]
+                    got = term if t == 0 else got + term
+                value.append(got)
+            inverse = 1.0 / value[1]
+            at = pl.ds(pl.multiple_of(c * width + r * LANES, LANES), LANES)
+            value_ref[0, :, at] = value[0] * inverse
+            value_ref[1, :, at] = inverse
+
     columns(0)
     columns(1)
+
+    @pl.loop(0, AHEAD)
+    def _(c):
+        columns(c + 2)
+        resample(c)
 
     @pl.loop(1, dev_count)
     def _(i):
@@ -191,106 +225,135 @@
     for e in range(exps):
         factor = jnp.where(exposure == e, jnp.minimum(own[e], clip_ratio * average) / own[e], factor)
 
-    def swapped(c):
-        return lax.div(lax.rem(c + SWAP_EVERY - 2, SWAP_EVERY), SWAP_EVERY - 1)
-
-    def stride_of(b, c):
-        if bits >= 3 and b == 1:
-            return 2 + 2 * swapped(c)
-        if bits >= 3 and b == 2:
-            return 4 - 2 * swapped(c)
-        return 1 << b
-
-    def bit_of(b, c):
-        return lax.rem(lax.div(me, stride_of(b, c)), 2)
-
-    def block_copy(b, c):
-        n = dev_count >> (b + 1)
-        bit = bit_of(b, c)
-        if b == 0:
-            source = partial_ref.at[lax.rem(c, ring), pl.ds((1 - bit) * n, n)]
-        else:
-            source = got_refs[b - 1].at[c, pl.ds((1 - bit) * n, n)]
+    def partner(stride):
+        return {"exp": me + (1 - 2 * lax.rem(lax.div(me, stride), 2)) * stride}
+
+    def stage_copy(b, c, late):
+        keep = dev_count >> (b + 1)
+        skip = 1 if b == 1 and not late else 0
+        source = partial_ref.at[lax.rem(c, ring)] if b == 0 else got_refs[b - 1].at[c]
         return pltpu.make_async_remote_copy(
-            src_ref=source,
-            dst_ref=got_refs[b].at[c],
+            src_ref=source.at[pl.ds(keep + skip, keep - skip)],
+            dst_ref=got_refs[b].at[c, pl.ds(skip, keep - skip)],
             send_sem=send_sem.at[b, c],
             recv_sem=recv_sem.at[b, c],
-            device_id={"exp": me + (1 - 2 * bit) * stride_of(b, c)},
+            device_id=partner(1 << bit_order(late)[b]),
             device_id_type=MESH,
         )
 
-    def kept(b, c):
-        n = dev_count >> (b + 1)
+    def last_copy(c):
+        keep = dev_count >> 2
+        return pltpu.make_async_remote_copy(
+            src_ref=got_refs[0].at[c, pl.ds(keep, 1)],
+            dst_ref=got_refs[1].at[c, pl.ds(0, 1)],
+            send_sem=last_send.at[c],
+            recv_sem=last_recv.at[c],
+            device_id=partner(2),
+            device_id_type=MESH,
+        )
+
+    def is_late(c):
+        return functools.reduce(lambda a, b: a | b, [c == late for late in LATE])
+
+    def merge(b, c, late):
+        keep = dev_count >> (b + 1)
+        stage_copy(b, c, late).wait_recv()
         if b == 0:
-            return partial_ref[lax.rem(c, ring), pl.ds(bit_of(b, c) * n, n)]
-        return got_refs[b - 1][c, pl.ds(bit_of(b, c) * n, n)]
-
-    @pl.loop(0, chunks + LAGS * bits - LAGS + 1)
+            got_refs[0][c] = got_refs[0][c] + partial_ref[lax.rem(c, ring), pl.ds(0, keep)]
+        elif b == 1 and not late:
+            at = pl.ds(1, keep - 1)
+            got_refs[1][c, at] = got_refs[1][c, at] + got_refs[0][c, at]
+        elif b == 2 and not late:
+            got_refs[2][c, pl.ds(0, 1)] = got_refs[2][c, pl.ds(0, 1)] + got_refs[0][c, pl.ds(0, 1)]
+            if keep > 1:
+                at = pl.ds(1, keep - 1)
+                got_refs[2][c, at] = got_refs[2][c, at] + got_refs[1][c, at]
+        elif b < bits - 1:
+            got_refs[b][c] = got_refs[b][c] + got_refs[b - 1][c, pl.ds(0, keep)]
+        if b < bits - 1:
+            stage_copy(b + 1, c, late).start()
+            return
+        total = got_refs[b][c, 0] + got_refs[b - 1][c, 0]
+        if not late:
+            last_copy(c).wait_recv()
+            total = total + got_refs[1][c, 0]
+        at = pl.ds(pl.multiple_of(c * width, LANES), width)
+        numerator = total[:tile_dev]
+        denominator = total[tile_dev:]
+        positive = denominator > 0
+        coadd_ref[:, at] = jnp.where(
+            positive, numerator / jnp.where(positive, denominator, 1.0), 0.0
+        )
+        depth_ref[:, at] = denominator
+
+    def produce(c):
+        for r in range(ROWS):
+            for kind in range(2):
+                at = pl.ds(pl.multiple_of(c * width + r * LANES, LANES), LANES)
+                piece_of = value_ref[kind, :, at] * factor
+                for part in range(PARTS):
+                    base = (kind * PARTS + part) * pad
+                    piece = piece_of.astype(jnp.bfloat16)
+                    parts_ref[base : base + rows, r * LANES : (r + 1) * LANES] = piece
+                    piece_of = piece_of - piece.astype(jnp.float32)
+
+        if ring < chunks:
+
+            @pl.when(c >= ring)
+            def _():
+                stage_copy(0, c - ring, False).wait_send()
+
+        added = jnp.dot(
+            pick_ref[is_late(c).astype(jnp.int32)],
+            parts_ref[...],
+            preferred_element_type=jnp.float32,
+        )
+        partial_ref[lax.rem(c, ring)] = added.reshape(dev_count, 2 * tile_dev, width)
+        stage_copy(0, c, False).start()
+
+    lags, late_lags = stage_lags(LAGS, bits), stage_lags(LATE_LAGS, bits)
+
+    @pl.loop(0, chunks + max(lags[-1], late_lags[-1]))
     def _(step):
+        @pl.when((step >= AHEAD) & (step < chunks))
+        def _():
+            columns(step + 2)
+            resample(step)
+
         @pl.when(step < chunks)
         def _():
-            c = step
-            columns(c + 2)
-            for r in range(ROWS):
-                value = []
-                for kind in range(2):
-                    mid = (cut_mid, var_mid)[kind]
-                    got = None
-                    for t in range(TAPS):
-                        from_row = c * ROWS + r + FIRST + t
-                        at = pl.ds(pl.multiple_of(from_row * LANES, LANES), LANES)
-                        term = taps_ref[0, kind, t] * mid[:, at]
-                        got = term if t == 0 else got + term
-                    value.append(got)
-                inverse = 1.0 / value[1]
-                scaled = value[0] * inverse
-                for kind in range(2):
-                    piece_of = (scaled, inverse)[kind] * factor
-                    for part in range(PARTS):
-                        base = (kind * PARTS + part) * pad
-                        piece = piece_of.astype(jnp.bfloat16)
-                        parts_ref[base : base + rows, r * LANES : (r + 1) * LANES] = piece
-                        piece_of = piece_of - piece.astype(jnp.float32)
-
-            @pl.when(c >= ring)
-            def _():
-                block_copy(0, c - ring).wait_send()
-
-            added = jnp.dot(
-                pick_ref[swapped(c)], parts_ref[...], preferred_element_type=jnp.float32
-            )
-            partial_ref[lax.rem(c, ring)] = added.reshape(dev_count, 2 * tile_dev, width)
-            block_copy(0, c).start()
-
-        for b in range(1, bits + 1):
-            c = step - (LAGS * (b - 1) + 1)
-
-            @pl.when((c >= 0) & (c < chunks))
-            def _(b=b, c=c):
-                block_copy(b - 1, c).wait_recv()
-                total = got_refs[b - 1][c] + kept(b - 1, c)
-                if b < bits:
-                    got_refs[b - 1][c] = total
-                    block_copy(b, c).start()
-                else:
-                    at = pl.ds(pl.multiple_of(c * width, LANES), width)
-                    numerator = total[0, :tile_dev]
-                    denominator = total[0, tile_dev:]
-                    positive = denominator > 0
-                    coadd_ref[:, at] = jnp.where(
-                        positive, numerator / jnp.where(positive, denominator, 1.0), 0.0
-                    )
-                    depth_ref[:, at] = denominator
+            produce(step)
+
+        for b in range(bits):
+            for late in (False, True):
+                c = step - (late_lags if late else lags)[b]
+                kind_here = is_late(c) if late else jnp.logical_not(is_late(c))
+
+                @pl.when((c >= 0) & (c < chunks) & kind_here)
+                def _(b=b, c=c, late=late):
+                    merge(b, c, late)
+
+        for i in range(LAST_PER_STEP):
+            c = (step - chunks) * LAST_PER_STEP + i
+
+            @pl.when((c >= 0) & (c < chunks) & jnp.logical_not(is_late(c)))
+            def _(c=c):
+                last_copy(c).start()
 
     @pl.loop(chunks - ring, chunks)
     def _(c):
-        block_copy(0, c).wait_send()
+        stage_copy(0, c, False).wait_send()
 
     @pl.loop(0, chunks)
     def _(c):
-        for b in range(1, bits):
-            block_copy(b, c).wait_send()
+        for late in (False, True):
+
+            @pl.when(is_late(c) if late else jnp.logical_not(is_late(c)))
+            def _(late=late):
+                for b in range(1, bits):
+                    stage_copy(b, c, late).wait_send()
+                if not late:
+                    last_copy(c).wait_send()
 
 
 def shards(cutouts, variance, offsets, correlation_tiles, slot_valid, tile_slot):
@@ -302,7 +365,7 @@
     bits = dev_count.bit_length() - 1
     chunks = P_SIZE // ROWS
     width = ROWS * P_SIZE
-    ring = min(chunks, 4)
+    ring = chunks if dev_count <= ALL_RING else min(chunks, 4)
     depth = 2 * PARTS * (-(-rows // PAD) * PAD)
     area = P_SIZE * P_SIZE
 
@@ -334,6 +397,7 @@
             pltpu.VMEM((2, 2, TAPS, rows, LANES), jnp.float32),
             pltpu.VMEM((rows, CP * P_SIZE), jnp.float32),
             pltpu.VMEM((rows, CP * P_SIZE), jnp.float32),
+            pltpu.VMEM((2, rows, area), jnp.float32),
             pltpu.VMEM((depth, 2 * tile_total), jnp.float32),
             pltpu.VMEM((2, 2 * tile_total, depth), jnp.bfloat16),
             pltpu.VMEM((depth, width), jnp.bfloat16),
@@ -349,6 +413,8 @@
             pltpu.SemaphoreType.DMA((dev_count,)),
             pltpu.SemaphoreType.DMA((bits, chunks)),
             pltpu.SemaphoreType.DMA((bits, chunks)),
+            pltpu.SemaphoreType.DMA((chunks,)),
+            pltpu.SemaphoreType.DMA((chunks,)),
         ],
         compiler_params=pltpu.CompilerParams(
             collective_id=0, has_side_effects=True, vmem_limit_bytes=VMEM_LIMIT

time: 64.9 us -> 60.7 us (0.935)
  Pallas kernels: 62.5 us -> 58.3 us
    pallas_call x1, Pallas kernels: 62.5 us -> 58.3 us  [shards(): pl.pallas_call(functools.partial(coadd_kernel, dev_count, bits, tile_tota...]
where the time goes in v2:
time: 60.7 us; the launch traced here: 60.5 us
  Pallas kernels  58.3 us (96%)
  local copies, waits for them, and re-layouts  0.82 us (1%)
  other arithmetic  0.74 us (1%)
  between operations  0.64 us (1%)
    pallas_call x1, Pallas kernels, shards(): pl.pallas_call(functools.partial(coadd_kernel, dev_count, bits, tile_tota...  58.3 us

profile of v2, /device:TPU:0, one launch (start us, length us, event | category | flops | bytes accessed | tf_op | source)
XLA Modules:
  0.0 60.5 jit_solution(3132648597095498040)
XLA Ops:
  0.6 0.7 %pad_add_fusion.small_ref = s32[9,128]{1,0:T(8,128)S(1)} fusion(s32[1,64]{1,0:T(1,128)} %bitcast.17, s32[2,12]{1,0:T(2,128)} %param.10, s32[2,12]{1,0:T(2,128)} %param.9, s32[4,12]{1,0:T(4,128)} %bitcast.16), kind=kLoop, calls=%fused_computation.2 | loop fusion | flops 3456 | bytes 5248 | tf_op jit(solution)/shard_map/concatenate | solution.py:373
  1.4 58.3 %coadd.1 = (f32[4,16384]{1,0:T(4,128)S(1)}, f32[4,16384]{1,0:T(4,128)S(1)}) custom-call(f32[12,2,20736]{2,1,0:T(2,128)} %bitcast.14, bf16[12,2,20736]{2,1,0:T(2,128)(2,1)} %bitcast.15, s32[9,128]{1,0:T(8,128)S(1)} %pad_add_fusion.small_ref), custom_call_target="tpu_custom_call" | custom-call | tf_op jit(solution)/shard_map/coadd/pallas_call | solution.py:387
  59.7 0.8 %copy_bitcast_fusion = (f32[4,128,128]{2,1,0:T(8,128)}, f32[4,128,128]{2,1,0:T(8,128)}) fusion(f32[1,4,128,128]{3,1,2,0:T(4,128)S(1)} %bitcast.13, f32[1,4,128,128]{3,1,2,0:T(4,128)S(1)} %bitcast.12), kind=kLoop, calls=%fused_computation | loop fusion | bytes 1048576 | tf_op jit(solution)/shard_map/reshape | solution.py:429

commit v3 on v2

--- a/solution.py
+++ b/solution.py
@@ -18,12 +18,15 @@
 PAD = 16
 PARTS = 2
 ALL_RING = 16
-AHEAD = 4
-LATE = (1,)
-LAGS = (1, 4, 8, 20)
-LATE_LAGS = (1, 3, 7, 16)
-LAST_PER_STEP = 3
+AHEAD = 3
+EARLY = 1
+LATE = (0, 2)
+LAGS = (1, 4, 7, 18)
+LATE_LAGS = (1, 6, 8, 19)
+LAST_FROM = 1
+LAST_PER_STEP = 4
 VMEM_LIMIT = 55_800_000
+VMEM_MOST = 60 * 1024 * 1024
 clip_ratio = 1.5
 MESH = pl.DeviceIdType.MESH
 
@@ -47,15 +50,19 @@
     return taps
 
 
+def unused(body):
+    return body
+
+
 def stage_lags(lags, bits):
     middle = [lags[2] + 4 * i for i in range(bits - 3)]
     return list(lags[:2]) + middle + [middle[-1] + lags[3] - lags[2]]
 
 
 def coadd_kernel(
-    dev_count, bits, slot_total, cut_hbm, var_hbm, small_ref,
+    dev_count, bits, slot_total, early, cut_hbm, var_hbm, small_ref,
     coadd_ref, depth_ref, cut_ref, var_ref, weight_src, weight_got, taps_ref,
-    cut_mid, var_mid, value_ref, pick_wide, pick_ref, parts_ref, partial_ref, *rest,
+    cut_mid, var_mid, value_ref, early_ref, early_got, pick_wide, pick_ref, parts_ref, partial_ref, *rest,
 ):
     got_refs = rest[:bits]
     load_sem, weight_send, weight_recv, send_sem, recv_sem, last_send, last_recv = rest[bits:]
@@ -66,7 +73,7 @@
     chunks = P_SIZE // ROWS
     span = ROWS * CP
     ring = partial_ref.shape[0]
-    pad = pick_wide.shape[0] // (2 * PARTS)
+    pad = pick_wide.shape[0] // PARTS
     me = lax.axis_index("exp")
 
     def bit_order(late):
@@ -125,8 +132,10 @@
         total = jnp.sum(jnp.where(exposure == e, row_total, 0.0), axis=0, keepdims=True)
         count = jnp.sum(jnp.where(exposure == e, valid, 0.0), axis=0, keepdims=True)
         own.append(1.0 / (total / (count * (CP * CP))))
-    own_sum = functools.reduce(lambda a, b: a + b, own)
-    weight_src[...] = jnp.broadcast_to(own_sum, weight_src.shape)
+    weight_row = lax.broadcasted_iota(jnp.int32, weight_src.shape, 0)
+    weight_src[...] = functools.reduce(
+        lambda a, b: a + b, [jnp.where(weight_row == e, own[e], 0.0) for e in range(exps)]
+    )
     pl.semaphore_wait(barrier, dev_count - 1)
 
     def weight_copy(i):
@@ -149,16 +158,35 @@
             taps_ref[axis, 0, t] = taps[t]
             taps_ref[axis, 1, t] = taps[t] * taps[t]
 
+    lane = lax.broadcasted_iota(jnp.int32, (rows, LANES), 1)
+
+    def shifted(blocks, by):
+        turned = [pltpu.roll(block, LANES - by, axis=1) for block in blocks]
+        return [
+            jnp.where(lane < LANES - by, here, beyond)
+            for here, beyond in zip(turned, turned[1:] + turned[-1:])
+        ]
+
     def columns(g):
         at = pl.ds(pl.multiple_of(g * span, LANES), span)
         for kind in range(2):
             data = (cut_ref, var_ref)[kind][:, at].astype(jnp.float32)
             mid = (cut_mid, var_mid)[kind]
+            first = [data[:, k * LANES : (k + 1) * LANES] for k in range(span // LANES)]
+            second, third = shifted(first, 1), shifted(first, 2)
+            tap = [taps_ref[1, kind, t] for t in range(TAPS)]
+            low, high = (
+                [tap[t] * x + tap[t + 1] * y + tap[t + 2] * z for x, y, z in zip(first, second, third)]
+                for t in (0, 3)
+            )
             for r in range(ROWS):
-                start = r * CP + FIRST
-                got = taps_ref[1, kind, 0] * data[:, start : start + LANES]
-                for t in range(1, TAPS):
-                    got = got + taps_ref[1, kind, t] * data[:, start + t : start + t + LANES]
+                got = None
+                for part, start in ((low, FIRST), (high, FIRST + 3)):
+                    block, by = divmod(r * CP + start, LANES)
+                    near = pltpu.roll(part[block], LANES - by, axis=1)
+                    far = pltpu.roll(part[block + 1], LANES - by, axis=1)
+                    term = jnp.where(lane < LANES - by, near, far)
+                    got = term if got is None else got + term
                 mid[:, pl.ds(pl.multiple_of((g * ROWS + r) * LANES, LANES), LANES)] = got
 
     row = lax.broadcasted_iota(jnp.int32, (rows, 2 * slot_total), 1)
@@ -183,7 +211,7 @@
         for kind in range(2):
             hit = jnp.where((kind_of == kind) & (wanted == storage), valid, 0.0)
             for part in range(PARTS):
-                base = (kind * PARTS + part) * pad
+                base = part * pad + kind * rows
                 pick_wide[base : base + rows, :] = hit
         pick_ref[late] = pick_wide[...].T.astype(jnp.bfloat16)
 
@@ -204,29 +232,78 @@
                 value.append(got)
             inverse = 1.0 / value[1]
             at = pl.ds(pl.multiple_of(c * width + r * LANES, LANES), LANES)
-            value_ref[0, :, at] = value[0] * inverse
-            value_ref[1, :, at] = inverse
+            value_ref[:rows, at] = value[0] * inverse
+            value_ref[rows:, at] = inverse
 
     columns(0)
     columns(1)
 
-    @pl.loop(0, AHEAD)
+    @pl.loop(0, early)
     def _(c):
         columns(c + 2)
         resample(c)
 
+    def partner(stride):
+        return {"exp": me + (1 - 2 * lax.rem(lax.div(me, stride), 2)) * stride}
+
+    def is_late(c):
+        return functools.reduce(lambda a, b: a | b, [c == late for late in LATE])
+
+    def partial_of(c, scale):
+        both = jnp.concatenate([scale, scale], axis=0)
+        for r in range(ROWS):
+            at = pl.ds(pl.multiple_of(c * width + r * LANES, LANES), LANES)
+            piece_of = value_ref[:, at] * both
+            for part in range(PARTS):
+                piece = piece_of.astype(jnp.bfloat16)
+                parts_ref[part * pad : part * pad + 2 * rows, r * LANES : (r + 1) * LANES] = piece
+                piece_of = piece_of - piece.astype(jnp.float32)
+        added = jnp.dot(
+            pick_ref[is_late(c).astype(jnp.int32)],
+            parts_ref[...],
+            preferred_element_type=jnp.float32,
+        )
+        return added.reshape(dev_count, 2 * tile_dev, width)
+
+    def early_copy(c):
+        half = dev_count // 2
+        return pltpu.make_async_remote_copy(
+            src_ref=early_ref.at[c, :, pl.ds(half, half)],
+            dst_ref=early_got.at[c],
+            send_sem=send_sem.at[0, c],
+            recv_sem=recv_sem.at[0, c],
+            device_id=partner(1),
+            device_id_type=MESH,
+        )
+
+    @pl.loop(0, early) if early else unused
+    def _(c):
+        for e in range(exps):
+            early_ref[c, e] = partial_of(c, jnp.where(exposure == e, 1.0, 0.0))
+        early_copy(c).start()
+
+    @pl.loop(early, AHEAD)
+    def _(c):
+        columns(c + 2)
+        resample(c)
+
     @pl.loop(1, dev_count)
     def _(i):
         weight_copy(i).wait()
 
     weight_got[0] = weight_src[...]
-    average = jnp.sum(weight_got[...], axis=0)[0:1, 0:1] / (exps * dev_count)
+    weight_sum = jnp.sum(jnp.sum(weight_got[...], axis=0), axis=0, keepdims=True)[:, 0:1]
+    average = weight_sum / (exps * dev_count)
+
+    def factor_of(weight):
+        return jnp.minimum(weight, clip_ratio * average) / weight
+
+    own_factor = [factor_of(own[e]) for e in range(exps)]
+    other = 1 + (dev_count - 2) * (1 - lax.rem(me, 2))
+    other_factor = [factor_of(weight_got[other, e : e + 1, 0:1]) for e in range(exps)]
     factor = jnp.zeros((rows, 1), jnp.float32)
     for e in range(exps):
-        factor = jnp.where(exposure == e, jnp.minimum(own[e], clip_ratio * average) / own[e], factor)
-
-    def partner(stride):
-        return {"exp": me + (1 - 2 * lax.rem(lax.div(me, stride), 2)) * stride}
+        factor = jnp.where(exposure == e, own_factor[e], factor)
 
     def stage_copy(b, c, late):
         keep = dev_count >> (b + 1)
@@ -252,8 +329,12 @@
             device_id_type=MESH,
         )
 
-    def is_late(c):
-        return functools.reduce(lambda a, b: a | b, [c == late for late in LATE])
+    def start_first(c):
+        for late in (False, True):
+
+            @pl.when(is_late(c) if late else jnp.logical_not(is_late(c)))
+            def _(late=late):
+                stage_copy(1, c, late).start()
 
     def merge(b, c, late):
         keep = dev_count >> (b + 1)
@@ -270,6 +351,9 @@
                 got_refs[2][c, at] = got_refs[2][c, at] + got_refs[1][c, at]
         elif b < bits - 1:
             got_refs[b][c] = got_refs[b][c] + got_refs[b - 1][c, pl.ds(0, keep)]
+        if b == 0:
+            start_first(c)
+            return
         if b < bits - 1:
             stage_copy(b + 1, c, late).start()
             return
@@ -287,29 +371,28 @@
         depth_ref[:, at] = denominator
 
     def produce(c):
-        for r in range(ROWS):
-            for kind in range(2):
-                at = pl.ds(pl.multiple_of(c * width + r * LANES, LANES), LANES)
-                piece_of = value_ref[kind, :, at] * factor
-                for part in range(PARTS):
-                    base = (kind * PARTS + part) * pad
-                    piece = piece_of.astype(jnp.bfloat16)
-                    parts_ref[base : base + rows, r * LANES : (r + 1) * LANES] = piece
-                    piece_of = piece_of - piece.astype(jnp.float32)
-
         if ring < chunks:
 
             @pl.when(c >= ring)
             def _():
                 stage_copy(0, c - ring, False).wait_send()
 
-        added = jnp.dot(
-            pick_ref[is_late(c).astype(jnp.int32)],
-            parts_ref[...],
-            preferred_element_type=jnp.float32,
-        )
-        partial_ref[lax.rem(c, ring)] = added.reshape(dev_count, 2 * tile_dev, width)
+        partial_ref[lax.rem(c, ring)] = partial_of(c, factor)
         stage_copy(0, c, False).start()
+
+    def merge_early(c):
+        early_copy(c).wait_recv()
+
+        @pl.loop(0, dev_count // 2)
+        def _(j):
+            total = None
+            for source, scale in ((early_ref, own_factor), (early_got, other_factor)):
+                for e in range(exps):
+                    term = source[c, e, j] * scale[e]
+                    total = term if total is None else total + term
+            got_refs[0][c, j] = total
+
+        start_first(c)
 
     lags, late_lags = stage_lags(LAGS, bits), stage_lags(LATE_LAGS, bits)
 
@@ -320,11 +403,19 @@
             columns(step + 2)
             resample(step)
 
-        @pl.when(step < chunks)
+        @pl.when((step >= early) & (step < chunks))
         def _():
             produce(step)
 
-        for b in range(bits):
+        @pl.when((step >= lags[0]) & (step < early + lags[0])) if early else unused
+        def _():
+            merge_early(step - lags[0])
+
+        @pl.when((step >= early + lags[0]) & (step < chunks + lags[0]))
+        def _():
+            merge(0, step - lags[0], False)
+
+        for b in range(1, bits):
             for late in (False, True):
                 c = step - (late_lags if late else lags)[b]
                 kind_here = is_late(c) if late else jnp.logical_not(is_late(c))
@@ -334,13 +425,17 @@
                     merge(b, c, late)
 
         for i in range(LAST_PER_STEP):
-            c = (step - chunks) * LAST_PER_STEP + i
+            c = (step - chunks - LAST_FROM) * LAST_PER_STEP + i
 
             @pl.when((c >= 0) & (c < chunks) & jnp.logical_not(is_late(c)))
             def _(c=c):
                 last_copy(c).start()
 
-    @pl.loop(chunks - ring, chunks)
+    @pl.loop(0, early) if early else unused
+    def _(c):
+        early_copy(c).wait_send()
+
+    @pl.loop(max(chunks - ring, early), chunks)
     def _(c):
         stage_copy(0, c, False).wait_send()
 
@@ -365,8 +460,13 @@
     bits = dev_count.bit_length() - 1
     chunks = P_SIZE // ROWS
     width = ROWS * P_SIZE
-    ring = chunks if dev_count <= ALL_RING else min(chunks, 4)
-    depth = 2 * PARTS * (-(-rows // PAD) * PAD)
+    roomy = dev_count <= ALL_RING
+    ring, early = (chunks, EARLY) if roomy else (min(chunks, 4), 0)
+    depth = PARTS * (-(-2 * rows // PAD) * PAD)
+
+    def early_shape(blocks):
+        return (early, exps, blocks, 2 * tile_dev, width) if early else (ROWS, LANES)
+
     area = P_SIZE * P_SIZE
 
     lanes = max(LANES, tile_total)
@@ -385,7 +485,7 @@
     whole = pl.BlockSpec(memory_space=pltpu.VMEM)
     far = pl.BlockSpec(memory_space=pltpu.HBM)
     coadd, depth_sum = pl.pallas_call(
-        functools.partial(coadd_kernel, dev_count, bits, tile_total),
+        functools.partial(coadd_kernel, dev_count, bits, tile_total, early),
         out_shape=(jax.ShapeDtypeStruct((tile_dev, area), jnp.float32),) * 2,
         in_specs=[far] * 2 + [whole],
         out_specs=(whole,) * 2,
@@ -397,7 +497,9 @@
             pltpu.VMEM((2, 2, TAPS, rows, LANES), jnp.float32),
             pltpu.VMEM((rows, CP * P_SIZE), jnp.float32),
             pltpu.VMEM((rows, CP * P_SIZE), jnp.float32),
-            pltpu.VMEM((2, rows, area), jnp.float32),
+            pltpu.VMEM((2 * rows, area), jnp.float32),
+            pltpu.VMEM(early_shape(dev_count), jnp.float32),
+            pltpu.VMEM(early_shape(dev_count // 2), jnp.float32),
             pltpu.VMEM((depth, 2 * tile_total), jnp.float32),
             pltpu.VMEM((2, 2 * tile_total, depth), jnp.bfloat16),
             pltpu.VMEM((depth, width), jnp.bfloat16),
@@ -417,7 +519,7 @@
             pltpu.SemaphoreType.DMA((chunks,)),
         ],
         compiler_params=pltpu.CompilerParams(
-            collective_id=0, has_side_effects=True, vmem_limit_bytes=VMEM_LIMIT
+            collective_id=0, has_side_effects=True, vmem_limit_bytes=VMEM_LIMIT if roomy else VMEM_MOST
         ),
         name="coadd",
     )(

time: 60.7 us -> 58.8 us (0.969)
  Pallas kernels: 58.3 us -> 56.5 us
    pallas_call x1, Pallas kernels: 58.3 us -> 56.5 us  [shards(): pl.pallas_call(functools.partial(coadd_kernel, dev_count, bits, tile_tota...]
where the time goes in v3:
time: 58.8 us; the launch traced here: 58.7 us
  Pallas kernels  56.5 us (96%)
  local copies, waits for them, and re-layouts  0.82 us (1%)
  other arithmetic  0.74 us (1%)
  between operations  0.64 us (1%)
    pallas_call x1, Pallas kernels, shards(): pl.pallas_call(functools.partial(coadd_kernel, dev_count, bits, tile_tota...  56.5 us

profile of v3, /device:TPU:0, one launch (start us, length us, event | category | flops | bytes accessed | tf_op | source)
XLA Modules:
  0.0 58.7 jit_solution(14368674048102298721)
XLA Ops:
  0.6 0.7 %pad_add_fusion.small_ref = s32[9,128]{1,0:T(8,128)S(1)} fusion(s32[1,64]{1,0:T(1,128)} %bitcast.17, s32[2,12]{1,0:T(2,128)} %param.10, s32[2,12]{1,0:T(2,128)} %param.9, s32[4,12]{1,0:T(4,128)} %bitcast.16), kind=kLoop, calls=%fused_computation.2 | loop fusion | flops 3456 | bytes 5248 | tf_op jit(solution)/shard_map/concatenate | solution.py:473
  1.4 56.5 %coadd.1 = (f32[4,16384]{1,0:T(4,128)S(1)}, f32[4,16384]{1,0:T(4,128)S(1)}) custom-call(f32[12,2,20736]{2,1,0:T(2,128)} %bitcast.14, bf16[12,2,20736]{2,1,0:T(2,128)(2,1)} %bitcast.15, s32[9,128]{1,0:T(8,128)S(1)} %pad_add_fusion.small_ref), custom_call_target="tpu_custom_call" | custom-call | tf_op jit(solution)/shard_map/coadd/pallas_call | solution.py:487
  57.8 0.8 %copy_bitcast_fusion = (f32[4,128,128]{2,1,0:T(8,128)}, f32[4,128,128]{2,1,0:T(8,128)}) fusion(f32[1,4,128,128]{3,1,2,0:T(4,128)S(1)} %bitcast.13, f32[1,4,128,128]{3,1,2,0:T(4,128)S(1)} %bitcast.12), kind=kLoop, calls=%fused_computation | loop fusion | bytes 1048576 | tf_op jit(solution)/shard_map/reshape | solution.py:531

commit v4 on v3

--- a/solution.py
+++ b/solution.py
@@ -19,11 +19,13 @@
 PARTS = 2
 ALL_RING = 16
 AHEAD = 3
-EARLY = 1
-LATE = (0, 2)
-LAGS = (1, 4, 7, 18)
-LATE_LAGS = (1, 6, 8, 19)
-LAST_FROM = 1
+RAW = 2
+RAW_AT = 4
+RAW_LAGS = (8, 14)
+LATE = (1, 4)
+LAGS = (1, 3, 6, 16)
+LATE_LAGS = (1, 5, 8, 16)
+LAST_FROM = -3
 LAST_PER_STEP = 4
 VMEM_LIMIT = 55_800_000
 VMEM_MOST = 60 * 1024 * 1024
@@ -50,22 +52,18 @@
     return taps
 
 
-def unused(body):
-    return body
-
-
 def stage_lags(lags, bits):
     middle = [lags[2] + 4 * i for i in range(bits - 3)]
     return list(lags[:2]) + middle + [middle[-1] + lags[3] - lags[2]]
 
 
 def coadd_kernel(
-    dev_count, bits, slot_total, early, cut_hbm, var_hbm, small_ref,
+    dev_count, bits, slot_total, raw, cut_hbm, var_hbm, small_ref,
     coadd_ref, depth_ref, cut_ref, var_ref, weight_src, weight_got, taps_ref,
-    cut_mid, var_mid, value_ref, early_ref, early_got, pick_wide, pick_ref, parts_ref, partial_ref, *rest,
+    cut_mid, var_mid, value_ref, raw_got, table_ref, table_got, pick_other, pick_wide, pick_ref, parts_ref, partial_ref, *rest,
 ):
     got_refs = rest[:bits]
-    load_sem, weight_send, weight_recv, send_sem, recv_sem, last_send, last_recv = rest[bits:]
+    load_sem, weight_send, weight_recv, send_sem, recv_sem, last_send, last_recv, raw_sem = rest[bits:]
     slots, exps, _ = cut_hbm.shape
     rows = slots * exps
     tile_dev = slot_total // dev_count
@@ -198,9 +196,7 @@
         axis=1,
         keepdims=True,
     )
-    pick_wide[...] = jnp.zeros_like(pick_wide)
-    parts_ref[...] = jnp.zeros_like(parts_ref)
-    for late in range(2):
+    def build_pick(late, stored, target):
         order = bit_order(late)
         owner = jnp.zeros_like(place)
         for b in range(bits):
@@ -209,12 +205,31 @@
             owner = owner + ((apart + mine) % 2) * (1 << order[b])
         wanted = (owner * tile_dev + row % tile_dev).astype(jnp.float32)
         for kind in range(2):
-            hit = jnp.where((kind_of == kind) & (wanted == storage), valid, 0.0)
+            hit = jnp.where((kind_of == kind) & (wanted == stored), 1.0, 0.0)
             for part in range(PARTS):
                 base = part * pad + kind * rows
                 pick_wide[base : base + rows, :] = hit
-        pick_ref[late] = pick_wide[...].T.astype(jnp.bfloat16)
-
+        target[late] = pick_wide[...].T.astype(jnp.bfloat16)
+
+    def partner(stride):
+        return {"exp": me + (1 - 2 * lax.rem(lax.div(me, stride), 2)) * stride}
+
+    def raw_copy(which, i):
+        at = pl.ds(pl.multiple_of(i * width, LANES), width)
+        return pltpu.make_async_remote_copy(
+            src_ref=(table_ref, value_ref.at[:, at])[which],
+            dst_ref=(table_got, raw_got)[which].at[i],
+            send_sem=raw_sem.at[2 * which, i],
+            recv_sem=raw_sem.at[2 * which + 1, i],
+            device_id=partner(2 + 2 * i),
+            device_id_type=MESH,
+        )
+
+    stored_here = jnp.where(valid > 0, storage, -1.0)
+    table_ref[...] = jnp.broadcast_to(stored_here, table_ref.shape)
+    if raw:
+        for i in range(RAW):
+            raw_copy(0, i).start()
     for s in range(slots):
         load(0, s).wait()
 
@@ -238,55 +253,46 @@
     columns(0)
     columns(1)
 
-    @pl.loop(0, early)
-    def _(c):
-        columns(c + 2)
-        resample(c)
-
-    def partner(stride):
-        return {"exp": me + (1 - 2 * lax.rem(lax.div(me, stride), 2)) * stride}
+    if raw:
+
+        @pl.loop(0, raw)
+        def _(c):
+            columns(c + 2)
+            resample(c)
+            raw_copy(1, c).start()
 
     def is_late(c):
         return functools.reduce(lambda a, b: a | b, [c == late for late in LATE])
 
-    def partial_of(c, scale):
+    def partial_of(read, scale, pick):
         both = jnp.concatenate([scale, scale], axis=0)
         for r in range(ROWS):
-            at = pl.ds(pl.multiple_of(c * width + r * LANES, LANES), LANES)
-            piece_of = value_ref[:, at] * both
+            piece_of = read(r) * both
             for part in range(PARTS):
                 piece = piece_of.astype(jnp.bfloat16)
                 parts_ref[part * pad : part * pad + 2 * rows, r * LANES : (r + 1) * LANES] = piece
                 piece_of = piece_of - piece.astype(jnp.float32)
-        added = jnp.dot(
-            pick_ref[is_late(c).astype(jnp.int32)],
-            parts_ref[...],
-            preferred_element_type=jnp.float32,
-        )
+        added = jnp.dot(pick, parts_ref[...], preferred_element_type=jnp.float32)
         return added.reshape(dev_count, 2 * tile_dev, width)
 
-    def early_copy(c):
-        half = dev_count // 2
-        return pltpu.make_async_remote_copy(
-            src_ref=early_ref.at[c, :, pl.ds(half, half)],
-            dst_ref=early_got.at[c],
-            send_sem=send_sem.at[0, c],
-            recv_sem=recv_sem.at[0, c],
-            device_id=partner(1),
-            device_id_type=MESH,
-        )
-
-    @pl.loop(0, early) if early else unused
-    def _(c):
-        for e in range(exps):
-            early_ref[c, e] = partial_of(c, jnp.where(exposure == e, 1.0, 0.0))
-        early_copy(c).start()
-
-    @pl.loop(early, AHEAD)
+    def own_values(c):
+        return lambda r: value_ref[:, pl.ds(pl.multiple_of(c * width + r * LANES, LANES), LANES)]
+
+    pick_wide[...] = jnp.zeros_like(pick_wide)
+    parts_ref[...] = jnp.zeros_like(parts_ref)
+    for late in range(2):
+        build_pick(late, stored_here, pick_ref)
+
+    @pl.loop(raw, AHEAD)
     def _(c):
         columns(c + 2)
         resample(c)
 
+    if raw:
+        for i in range(RAW):
+            raw_copy(0, i).wait_recv()
+            build_pick(i, table_got[i, :, 0:1], pick_other)
+
     @pl.loop(1, dev_count)
     def _(i):
         weight_copy(i).wait()
@@ -298,12 +304,17 @@
     def factor_of(weight):
         return jnp.minimum(weight, clip_ratio * average) / weight
 
-    own_factor = [factor_of(own[e]) for e in range(exps)]
-    other = 1 + (dev_count - 2) * (1 - lax.rem(me, 2))
-    other_factor = [factor_of(weight_got[other, e : e + 1, 0:1]) for e in range(exps)]
-    factor = jnp.zeros((rows, 1), jnp.float32)
-    for e in range(exps):
-        factor = jnp.where(exposure == e, own_factor[e], factor)
+    def spread(weights):
+        column = jnp.zeros((rows, 1), jnp.float32)
+        for e in range(exps):
+            column = jnp.where(exposure == e, factor_of(weights[e]), column)
+        return column
+
+    def weights_of(stride):
+        i = stride + (dev_count - 2 * stride) * (1 - lax.rem(lax.div(me, stride), 2))
+        return [weight_got[i, e : e + 1, 0:1] for e in range(exps)]
+
+    factor = spread(own)
 
     def stage_copy(b, c, late):
         keep = dev_count >> (b + 1)
@@ -336,7 +347,7 @@
             def _(late=late):
                 stage_copy(1, c, late).start()
 
-    def merge(b, c, late):
+    def merge(b, c, late, whole=False):
         keep = dev_count >> (b + 1)
         stage_copy(b, c, late).wait_recv()
         if b == 0:
@@ -344,7 +355,7 @@
         elif b == 1 and not late:
             at = pl.ds(1, keep - 1)
             got_refs[1][c, at] = got_refs[1][c, at] + got_refs[0][c, at]
-        elif b == 2 and not late:
+        elif b == 2 and not late and not whole:
             got_refs[2][c, pl.ds(0, 1)] = got_refs[2][c, pl.ds(0, 1)] + got_refs[0][c, pl.ds(0, 1)]
             if keep > 1:
                 at = pl.ds(1, keep - 1)
@@ -358,7 +369,7 @@
             stage_copy(b + 1, c, late).start()
             return
         total = got_refs[b][c, 0] + got_refs[b - 1][c, 0]
-        if not late:
+        if not late and not whole:
             last_copy(c).wait_recv()
             total = total + got_refs[1][c, 0]
         at = pl.ds(pl.multiple_of(c * width, LANES), width)
@@ -377,69 +388,109 @@
             def _():
                 stage_copy(0, c - ring, False).wait_send()
 
-        partial_ref[lax.rem(c, ring)] = partial_of(c, factor)
+        pick = pick_ref[is_late(c).astype(jnp.int32)]
+        partial_ref[lax.rem(c, ring)] = partial_of(own_values(c), factor, pick)
         stage_copy(0, c, False).start()
 
-    def merge_early(c):
-        early_copy(c).wait_recv()
-
-        @pl.loop(0, dev_count // 2)
-        def _(j):
-            total = None
-            for source, scale in ((early_ref, own_factor), (early_got, other_factor)):
-                for e in range(exps):
-                    term = source[c, e, j] * scale[e]
-                    total = term if total is None else total + term
-            got_refs[0][c, j] = total
-
-        start_first(c)
+    def raw_core(i):
+        quarter = dev_count // 4
+        return pltpu.make_async_remote_copy(
+            src_ref=partial_ref.at[i, pl.ds(dev_count // 2, quarter)],
+            dst_ref=got_refs[1].at[i],
+            send_sem=send_sem.at[0, i],
+            recv_sem=recv_sem.at[0, i],
+            device_id=partner(1),
+            device_id_type=MESH,
+        )
+
+    def raw_produce(i):
+        partial_ref[i] = partial_of(own_values(i), factor, pick_ref[i])
+        raw_copy(1, i).wait_recv()
+        there = spread(weights_of(2 + 2 * i))
+        added = partial_of(
+            lambda r: raw_got[i, :, r * LANES : (r + 1) * LANES], there, pick_other[i]
+        )
+        partial_ref[i] = partial_ref[i] + added
+        raw_core(i).start()
+
+    def raw_merge(i):
+        raw_core(i).wait_recv()
+        got_refs[1][i] = got_refs[1][i] + partial_ref[i, pl.ds(0, dev_count // 4)]
+        stage_copy(2, i, bool(i)).start()
 
     lags, late_lags = stage_lags(LAGS, bits), stage_lags(LATE_LAGS, bits)
+    first = 1 - raw
+
+    def is_split(c):
+        return jnp.logical_not(is_late(c)) & (c >= raw)
 
     @pl.loop(0, chunks + max(lags[-1], late_lags[-1]))
     def _(step):
-        @pl.when((step >= AHEAD) & (step < chunks))
+        made = step + raw
+
+        @pl.when((made >= AHEAD) & (made < chunks))
         def _():
-            columns(step + 2)
-            resample(step)
-
-        @pl.when((step >= early) & (step < chunks))
+            columns(made + 2)
+            resample(made)
+
+        @pl.when(made < chunks)
         def _():
-            produce(step)
-
-        @pl.when((step >= lags[0]) & (step < early + lags[0])) if early else unused
+            produce(made)
+
+        @pl.when((step >= raw + first) & (step < chunks + first))
         def _():
-            merge_early(step - lags[0])
-
-        @pl.when((step >= early + lags[0]) & (step < chunks + lags[0]))
-        def _():
-            merge(0, step - lags[0], False)
+            merge(0, step - first, False)
+
+        if raw:
+            for i in range(RAW):
+
+                @pl.when(step == RAW_AT)
+                def _(i=i):
+                    raw_produce(i)
+
+            for i in range(RAW):
+
+                @pl.when(step == RAW_AT + 1)
+                def _(i=i):
+                    raw_merge(i)
+
+            for b in range(2, bits):
+
+                @pl.when(step == RAW_LAGS[b - 2])
+                def _(b=b):
+                    merge(b, 0, False, True)
 
         for b in range(1, bits):
             for late in (False, True):
                 c = step - (late_lags if late else lags)[b]
-                kind_here = is_late(c) if late else jnp.logical_not(is_late(c))
-
-                @pl.when((c >= 0) & (c < chunks) & kind_here)
+                here = is_late(c) if late else is_split(c)
+                if late and b == 1:
+                    here = here & (c >= raw)
+
+                @pl.when((c >= 0) & (c < chunks) & here)
                 def _(b=b, c=c, late=late):
                     merge(b, c, late)
 
         for i in range(LAST_PER_STEP):
             c = (step - chunks - LAST_FROM) * LAST_PER_STEP + i
 
-            @pl.when((c >= 0) & (c < chunks) & jnp.logical_not(is_late(c)))
+            @pl.when((c >= 0) & (c < chunks) & is_split(c))
             def _(c=c):
                 last_copy(c).start()
 
-    @pl.loop(0, early) if early else unused
-    def _(c):
-        early_copy(c).wait_send()
-
-    @pl.loop(max(chunks - ring, early), chunks)
+    if raw:
+        for i in range(RAW):
+            raw_core(i).wait_send()
+            for which in range(2):
+                raw_copy(which, i).wait_send()
+            for b in range(2, bits):
+                stage_copy(b, i, bool(i)).wait_send()
+
+    @pl.loop(max(chunks - ring, raw), chunks)
     def _(c):
         stage_copy(0, c, False).wait_send()
 
-    @pl.loop(0, chunks)
+    @pl.loop(raw, chunks)
     def _(c):
         for late in (False, True):
 
@@ -461,11 +512,8 @@
     chunks = P_SIZE // ROWS
     width = ROWS * P_SIZE
     roomy = dev_count <= ALL_RING
-    ring, early = (chunks, EARLY) if roomy else (min(chunks, 4), 0)
+    ring, raw = (chunks, RAW) if roomy else (min(chunks, 4), 0)
     depth = PARTS * (-(-2 * rows // PAD) * PAD)
-
-    def early_shape(blocks):
-        return (early, exps, blocks, 2 * tile_dev, width) if early else (ROWS, LANES)
 
     area = P_SIZE * P_SIZE
 
@@ -485,7 +533,7 @@
     whole = pl.BlockSpec(memory_space=pltpu.VMEM)
     far = pl.BlockSpec(memory_space=pltpu.HBM)
     coadd, depth_sum = pl.pallas_call(
-        functools.partial(coadd_kernel, dev_count, bits, tile_total, early),
+        functools.partial(coadd_kernel, dev_count, bits, tile_total, raw),
         out_shape=(jax.ShapeDtypeStruct((tile_dev, area), jnp.float32),) * 2,
         in_specs=[far] * 2 + [whole],
         out_specs=(whole,) * 2,
@@ -498,8 +546,10 @@
             pltpu.VMEM((rows, CP * P_SIZE), jnp.float32),
             pltpu.VMEM((rows, CP * P_SIZE), jnp.float32),
             pltpu.VMEM((2 * rows, area), jnp.float32),
-            pltpu.VMEM(early_shape(dev_count), jnp.float32),
-            pltpu.VMEM(early_shape(dev_count // 2), jnp.float32),
+            pltpu.VMEM((RAW, 2 * rows, width), jnp.float32),
+            pltpu.VMEM((rows, LANES), jnp.float32),
+            pltpu.VMEM((RAW, rows, LANES), jnp.float32),
+            pltpu.VMEM((2, 2 * tile_total, depth), jnp.bfloat16),
             pltpu.VMEM((depth, 2 * tile_total), jnp.float32),
             pltpu.VMEM((2, 2 * tile_total, depth), jnp.bfloat16),
             pltpu.VMEM((depth, width), jnp.bfloat16),
@@ -517,6 +567,7 @@
             pltpu.SemaphoreType.DMA((bits, chunks)),
             pltpu.SemaphoreType.DMA((chunks,)),
             pltpu.SemaphoreType.DMA((chunks,)),
+            pltpu.SemaphoreType.DMA((4, RAW)),
         ],
         compiler_params=pltpu.CompilerParams(
             collective_id=0, has_side_effects=True, vmem_limit_bytes=VMEM_LIMIT if roomy else VMEM_MOST

time: 58.8 us -> 57.7 us (0.981)
  Pallas kernels: 56.5 us -> 55.4 us
    pallas_call x1, Pallas kernels: 56.5 us -> 55.4 us  [shards(): pl.pallas_call(functools.partial(coadd_kernel, dev_count, bits, tile_tota...]
where the time goes in v4:
time: 57.7 us; the launch traced here: 57.6 us
  Pallas kernels  55.4 us (96%)
  local copies, waits for them, and re-layouts  0.82 us (1%)
  other arithmetic  0.74 us (1%)
  between operations  0.64 us (1%)
    pallas_call x1, Pallas kernels, shards(): pl.pallas_call(functools.partial(coadd_kernel, dev_count, bits, tile_tota...  55.4 us

profile of v4, /device:TPU:0, one launch (start us, length us, event | category | flops | bytes accessed | tf_op | source)
XLA Modules:
  0.0 57.6 jit_solution(2784291113384893470)
XLA Ops:
  0.6 0.7 %pad_add_fusion.small_ref = s32[9,128]{1,0:T(8,128)S(1)} fusion(s32[1,64]{1,0:T(1,128)} %bitcast.17, s32[2,12]{1,0:T(2,128)} %param.10, s32[2,12]{1,0:T(2,128)} %param.9, s32[4,12]{1,0:T(4,128)} %bitcast.16), kind=kLoop, calls=%fused_computation.2 | loop fusion | flops 3456 | bytes 5248 | tf_op jit(solution)/shard_map/concatenate | solution.py:521
  1.4 55.4 %coadd.1 = (f32[4,16384]{1,0:T(4,128)S(1)}, f32[4,16384]{1,0:T(4,128)S(1)}) custom-call(f32[12,2,20736]{2,1,0:T(2,128)} %bitcast.14, bf16[12,2,20736]{2,1,0:T(2,128)(2,1)} %bitcast.15, s32[9,128]{1,0:T(8,128)S(1)} %pad_add_fusion.small_ref), custom_call_target="tpu_custom_call" | custom-call | tf_op jit(solution)/shard_map/coadd/pallas_call | solution.py:535
  56.7 0.8 %copy_bitcast_fusion = (f32[4,128,128]{2,1,0:T(8,128)}, f32[4,128,128]{2,1,0:T(8,128)}) fusion(f32[1,4,128,128]{3,1,2,0:T(4,128)S(1)} %bitcast.13, f32[1,4,128,128]{3,1,2,0:T(4,128)S(1)} %bitcast.12), kind=kLoop, calls=%fused_computation | loop fusion | bytes 1048576 | tf_op jit(solution)/shard_map/reshape | solution.py:582

commit v5 on v4

--- a/solution.py
+++ b/solution.py
@@ -25,8 +25,8 @@
 LATE = (1, 4)
 LAGS = (1, 3, 6, 16)
 LATE_LAGS = (1, 5, 8, 16)
-LAST_FROM = -3
-LAST_PER_STEP = 4
+LAST_FROM = -2
+LAST_PER_STEP = 3
 VMEM_LIMIT = 55_800_000
 VMEM_MOST = 60 * 1024 * 1024
 clip_ratio = 1.5
@@ -79,21 +79,23 @@
 
     barrier = pltpu.get_barrier_semaphore()
 
+    def load(kind, s):
+        source, to = ((cut_hbm, cut_ref), (var_hbm, var_ref))[kind]
+        return pltpu.make_async_copy(
+            source.at[s], to.at[pl.ds(s * exps, exps)], load_sem.at[kind, s]
+        )
+
+    for s in range(slots):
+        load(1, s).start()
+
     @pl.loop(1, dev_count)
     def _(i):
         pl.semaphore_signal(
             barrier, inc=1, device_id={"exp": lax.rem(me + i, dev_count)}, device_id_type=MESH
         )
 
-    def load(kind, s):
-        source, to = ((cut_hbm, cut_ref), (var_hbm, var_ref))[kind]
-        return pltpu.make_async_copy(
-            source.at[s], to.at[pl.ds(s * exps, exps)], load_sem.at[kind, s]
-        )
-
-    for kind in (1, 0):
-        for s in range(slots):
-            load(kind, s).start()
+    for s in range(slots):
+        load(0, s).start()
 
     of_row = lax.broadcasted_iota(jnp.int32, (rows, slots), 0)
     of_slot = lax.broadcasted_iota(jnp.int32, (rows, slots), 1) == of_row // exps

time: 57.7 us -> 57.6 us (level)
  no operation moved by 1% of the time
where the time goes in v5:
time: 57.6 us; the launch traced here: 57.4 us
  Pallas kernels  55.2 us (96%)
  local copies, waits for them, and re-layouts  0.82 us (1%)
  other arithmetic  0.74 us (1%)
  between operations  0.64 us (1%)
    pallas_call x1, Pallas kernels, shards(): pl.pallas_call(functools.partial(coadd_kernel, dev_count, bits, tile_tota...  55.2 us

profile of v5, /device:TPU:0, one launch (start us, length us, event | category | flops | bytes accessed | tf_op | source)
XLA Modules:
  0.0 57.4 jit_solution(345065782820726552)
XLA Ops:
  0.6 0.7 %pad_add_fusion.small_ref = s32[9,128]{1,0:T(8,128)S(1)} fusion(s32[1,64]{1,0:T(1,128)} %bitcast.17, s32[2,12]{1,0:T(2,128)} %param.10, s32[2,12]{1,0:T(2,128)} %param.9, s32[4,12]{1,0:T(4,128)} %bitcast.16), kind=kLoop, calls=%fused_computation.2 | loop fusion | flops 3456 | bytes 5248 | tf_op jit(solution)/shard_map/concatenate | solution.py:523
  1.4 55.2 %coadd.1 = (f32[4,16384]{1,0:T(4,128)S(1)}, f32[4,16384]{1,0:T(4,128)S(1)}) custom-call(f32[12,2,20736]{2,1,0:T(2,128)} %bitcast.14, bf16[12,2,20736]{2,1,0:T(2,128)(2,1)} %bitcast.15, s32[9,128]{1,0:T(8,128)S(1)} %pad_add_fusion.small_ref), custom_call_target="tpu_custom_call" | custom-call | tf_op jit(solution)/shard_map/coadd/pallas_call | solution.py:537
  56.6 0.8 %copy_bitcast_fusion = (f32[4,128,128]{2,1,0:T(8,128)}, f32[4,128,128]{2,1,0:T(8,128)}) fusion(f32[1,4,128,128]{3,1,2,0:T(4,128)S(1)} %bitcast.13, f32[1,4,128,128]{3,1,2,0:T(4,128)S(1)} %bitcast.12), kind=kLoop, calls=%fused_computation | loop fusion | bytes 1048576 | tf_op jit(solution)/shard_map/reshape | solution.py:584
